TPU v7x, 32 devices: a whole 2x2x4 slice. The times are simulated.
32 devices in a mesh: dp: 2 (over x), tp: 4 (over z), ep: 4 (over y, core).
Axes of the slice: x: 2, y: 2, z: 4, core: 2. Of those that a mesh axis runs over, the one named last changes fastest.
Arguments:
- hidden: bfloat16 [1024, 768], P(('dp', 'ep')), parts along dimension 0
- write_pos: int32 [1024], P(('dp', 'ep')), parts along dimension 0
- enc_mask: int32 [1024, 128], P(('dp', 'ep')), parts along dimension 0
- expert_idx: int32 [1024], P(('dp', 'ep')), parts along dimension 0
- self_keys: bfloat16 [2, 1024, 12, 32, 64], P(None, ('dp', 'ep'), 'tp'), parts along dimension 1
- self_values: bfloat16 [2, 1024, 12, 32, 64], P(None, ('dp', 'ep'), 'tp'), parts along dimension 1
- cross_keys: bfloat16 [2, 1024, 12, 128, 64], P(None, ('dp', 'ep'), 'tp'), parts along dimension 1
- cross_values: bfloat16 [2, 1024, 12, 128, 64], P(None, ('dp', 'ep'), 'tp'), parts along dimension 1
- rel_bias: float32 [12, 32], P('tp')
- norm_scale: float32 [2, 3, 768], replicated
- w_query: bfloat16 [2, 768, 768], P(None, None, 'tp')
- w_key: bfloat16 [2, 768, 768], P(None, None, 'tp')
- w_value: bfloat16 [2, 768, 768], P(None, None, 'tp')
- w_out: bfloat16 [2, 768, 768], P(None, 'tp')
- w_cross_query: bfloat16 [2, 768, 768], P(None, None, 'tp')
- w_cross_out: bfloat16 [2, 768, 768], P(None, 'tp')
- dense_gate: bfloat16 [768, 3072], P(None, 'tp')
- dense_up: bfloat16 [768, 3072], P(None, 'tp')
- dense_down: bfloat16 [3072, 768], P('tp')
- router: float32 [768, 8], replicated
- exp_gate: bfloat16 [8, 768, 3072], P('ep', None, 'tp')
- exp_up: bfloat16 [8, 768, 3072], P('ep', None, 'tp')
- exp_down: bfloat16 [8, 3072, 768], P('ep', 'tp')
Outputs:
- output 1: bfloat16 [1024, 768], P(('dp', 'ep')), parts along dimension 0
- output 2: bfloat16 [2, 1024, 12, 32, 64], P(None, ('dp', 'ep'), 'tp'), parts along dimension 1
- output 3: bfloat16 [2, 1024, 12, 32, 64], P(None, ('dp', 'ep'), 'tp'), parts along dimension 1
There are 2 independent parts. A program takes and returns all parts, laid end to end along the dimension named above; an argument that names none is the same for every part.
All inputs are finite; a program needn't handle non-finite values.
Results may differ from a plain program's by a relative error of at most 0.02.
Values are sent between devices in bfloat16 or wider.
A program may use at most 1 GiB of HBM per device.

v0:
```python
import jax
import jax.numpy as jnp
from jax import lax
from jax.sharding import PartitionSpec as P

EPS = 1e-6
NEG_BIG = -1e9


def rms_norm(h_cur, scale):
    h_float = h_cur.astype(jnp.float32)
    inv_rms = lax.rsqrt(jnp.mean(h_float * h_float, axis=-1, keepdims=True) + EPS)
    return (h_float * inv_rms * scale).astype(jnp.bfloat16)


def add_residual(h_cur, delta):
    return (h_cur.astype(jnp.float32) + delta.astype(jnp.float32)).astype(jnp.bfloat16)


def project(normed, weight):
    return jnp.dot(normed, weight, preferred_element_type=jnp.float32)


def self_attention(normed, write_pos, keys, values, w_query, w_key, w_value, w_out, rel_bias):
    tokens = normed.shape[0]
    heads, cache_len = rel_bias.shape
    head_dim = keys.shape[-1]
    query = project(normed, w_query).astype(jnp.bfloat16).reshape(tokens, heads, head_dim)
    key_new = project(normed, w_key).astype(jnp.bfloat16).reshape(tokens, heads, head_dim)
    value_new = project(normed, w_value).astype(jnp.bfloat16).reshape(tokens, heads, head_dim)
    distance = write_pos[:, None] - jnp.arange(cache_len)[None, :]
    at_slot = (distance == 0)[:, None, :, None]
    keys = jnp.where(at_slot, key_new[:, :, None, :], keys)
    values = jnp.where(at_slot, value_new[:, :, None, :], values)
    scores = jnp.einsum('thd,thld->thl', query, keys, preferred_element_type=jnp.float32)
    bias = jnp.take(rel_bias, jnp.maximum(distance, 0), axis=1)
    scores = jnp.where((distance >= 0)[:, None, :], scores + jnp.swapaxes(bias, 0, 1), NEG_BIG)
    attn_prob = jax.nn.softmax(scores, axis=-1).astype(jnp.bfloat16)
    context = jnp.einsum('thl,thld->thd', attn_prob, values, preferred_element_type=jnp.float32).astype(jnp.bfloat16)
    return project(context.reshape(tokens, heads * head_dim), w_out), keys, values


def cross_attention(normed, enc_mask, keys, values, w_query, w_out):
    tokens = normed.shape[0]
    heads = keys.shape[1]
    head_dim = keys.shape[-1]
    query = project(normed, w_query).astype(jnp.bfloat16).reshape(tokens, heads, head_dim)
    scores = jnp.einsum('thd,thsd->ths', query, keys, preferred_element_type=jnp.float32)
    scores = jnp.where((enc_mask > 0)[:, None, :], scores, NEG_BIG)
    attn_prob = jax.nn.softmax(scores, axis=-1).astype(jnp.bfloat16)
    context = jnp.einsum('ths,thsd->thd', attn_prob, values, preferred_element_type=jnp.float32).astype(jnp.bfloat16)
    return project(context.reshape(tokens, heads * head_dim), w_out)


def gated_ffn(normed, w_gate, w_up, w_down):
    product = (jax.nn.gelu(project(normed, w_gate)) * project(normed, w_up)).astype(jnp.bfloat16)
    return project(product, w_down)


def switch_layer(normed, expert_idx, router, exp_gate, exp_up, exp_down):
    tokens = normed.shape[0]
    experts = router.shape[1]
    capacity = (2 * tokens + experts - 1) // experts
    logits = jnp.dot(normed.astype(jnp.float32), router, preferred_element_type=jnp.float32)
    route_prob = jax.nn.softmax(logits, axis=-1)
    onehot = (expert_idx[:, None] == jnp.arange(experts)[None, :]).astype(jnp.int32)
    gate = jnp.sum(route_prob * onehot, axis=-1)
    slot = jnp.sum((jnp.cumsum(onehot, axis=0) - onehot) * onehot, axis=-1)
    dispatch = (onehot[:, :, None] * (slot[:, None, None] == jnp.arange(capacity)[None, None, :])).astype(jnp.bfloat16)
    buffers = jnp.einsum('tec,td->ecd', dispatch, normed, preferred_element_type=jnp.float32).astype(jnp.bfloat16)
    received = lax.all_to_all(buffers, 'ep', 0, 1, tiled=True)
    gate_in = jnp.einsum('ecd,edf->ecf', received, exp_gate, preferred_element_type=jnp.float32)
    lin_in = jnp.einsum('ecd,edf->ecf', received, exp_up, preferred_element_type=jnp.float32)
    product = (jax.nn.gelu(gate_in) * lin_in).astype(jnp.bfloat16)
    expert_out = jnp.einsum('ecf,efd->ecd', product, exp_down, preferred_element_type=jnp.float32).astype(jnp.bfloat16)
    expert_out = lax.psum(expert_out, 'tp')
    returned = lax.all_to_all(expert_out, 'ep', 1, 0, tiled=True)
    combined = jnp.einsum('tec,ecd->td', dispatch, returned, preferred_element_type=jnp.float32)
    return gate[:, None] * combined


def decode_body(hidden, write_pos, enc_mask, expert_idx, self_keys, self_values, cross_keys, cross_values, rel_bias, norm_scale, w_query, w_key, w_value, w_out, w_cross_query, w_cross_out, dense_gate, dense_up, dense_down, router, exp_gate, exp_up, exp_down):
    h_cur = hidden
    keys_list = []
    values_list = []
    for layer in range(2):
        normed = rms_norm(h_cur, norm_scale[layer, 0])
        attn_part, keys_new, values_new = self_attention(normed, write_pos, self_keys[layer], self_values[layer], w_query[layer], w_key[layer], w_value[layer], w_out[layer], rel_bias)
        h_cur = add_residual(h_cur, lax.psum(attn_part.astype(jnp.bfloat16), 'tp'))
        keys_list.append(keys_new)
        values_list.append(values_new)
        normed = rms_norm(h_cur, norm_scale[layer, 1])
        cross_part = cross_attention(normed, enc_mask, cross_keys[layer], cross_values[layer], w_cross_query[layer], w_cross_out[layer])
        h_cur = add_residual(h_cur, lax.psum(cross_part.astype(jnp.bfloat16), 'tp'))
        normed = rms_norm(h_cur, norm_scale[layer, 2])
        if layer == 0:
            ffn_part = gated_ffn(normed, dense_gate, dense_up, dense_down)
            h_cur = add_residual(h_cur, lax.psum(ffn_part.astype(jnp.bfloat16), 'tp'))
        else:
            h_cur = add_residual(h_cur, switch_layer(normed, expert_idx, router, exp_gate, exp_up, exp_down))
    return h_cur, jnp.stack(keys_list), jnp.stack(values_list)


def solution(mesh):
    batch = ('dp', 'ep')
    row_spec = P(batch, None)
    vec_spec = P(batch)
    cache_spec = P(None, batch, 'tp', None, None)
    col_spec = P(None, None, 'tp')
    out_rows = P(None, 'tp', None)
    in_specs = (row_spec, vec_spec, row_spec, vec_spec, cache_spec, cache_spec, cache_spec, cache_spec, P('tp', None), P(), col_spec, col_spec, col_spec, out_rows, col_spec, out_rows, P(None, 'tp'), P(None, 'tp'), P('tp', None), P(), P('ep', None, 'tp'), P('ep', None, 'tp'), P('ep', 'tp', None))
    out_specs = (row_spec, cache_spec, cache_spec)
    return jax.shard_map(decode_body, mesh=mesh, in_specs=in_specs, out_specs=out_specs, check_vma=False)
```

profile of v0, /device:TPU:0, one launch (start us, length us, event | category | flops | bytes accessed | tf_op | source)
XLA Modules:
  0.0 360.0 jit_solution(16609143580999358955)
XLA Ops:
  7.2 0.9 fusion.137
  8.2 0.7 fusion.135
  8.9 1.0 fusion.53
  10.0 0.8 copy.49
  10.7 1.4 slice_reduce_fusion
  12.1 1.4 convolution_convert_fusion.13
  13.5 1.4 convolution_convert_fusion.12
  15.0 1.4 convolution_convert_fusion.14
  16.6 2.1 multiply_reduce_fusion.3
  18.6 2.9 copy.62
  21.5 14.2 %gather_fusion = f32[4096,3]{1,0:T(8,128)} fusion(f32[3,32]{0,1:T(8,128)S(1)} %copy.49, s32[4096]{0:T(1024)S(1)} %broadcast_clamp_fusion), kind=kCustom, calls=%fused_computation.clone | custom fusion | bytes 114688 | tf_op jit(solution)/shard_map/jit(_take)/gather | solution.py:36
  35.7 5.0 %fusion.24 = f32[128,3,32]{1,2,0:T(8,128)} fusion(f32[128,3,32]{1,2,0:T(8,128)} %copy.62, f32[128,32,3]{2,1,0:T(8,128)} %bitcast.192, pred[128,32]{1,0:T(8,128)(4,1)S(1)} %get-tuple-element.23, pred[128,32]{1,0:T(8,128)(4,1)S(1)} %get-tuple-element.22), kind=kOutput, calls=%fused_computation.45 | output fusion | flops 86846 | bytes 155648 | tf_op jit(solution)/shard_map/div | solution.py:38
  40.8 2.7 copy.89
  43.5 1.9 multiply_reduce_fusion.2
  45.4 0.9 convolution_convert_fusion.6
  46.5 37.6 %all-reduce.7.cloned.1.call-done = bf16[128,768]{1,0:T(8,128)(2,1)} async-done(((bf16[128,768]{1,0:T(8,128)(2,1)}), bf16[128,768]{1,0:T(8,128)(2,1)}) %all-reduce.7.cloned.1.call-update) | async-done | bytes 196624 | tf_op jit(solution)/shard_map/psum | solution.py:89
  84.1 1.1 fusion.57
  85.2 1.4 convolution_convert_fusion.11
  86.7 5.2 %fusion.14 = f32[128,3,1,128]{3,2,1,0:T(1,128)} fusion(bf16[128,3,64,1]{2,3,1,0:T(2,128)(2,1)S(1)} %copy.68, bf16[2,128,3,128,64]{3,4,2,1,0:T(8,128)(2,1)} %param.31), kind=kOutput, calls=%fused_computation.15 | convolution fusion | flops 6291456 | bytes 6537216 | tf_op jit(solution)/shard_map/thd,thsd->ths/dot_general | solution.py:48
  91.9 1.8 fusion.39
  93.7 6.2 %fusion.12 = bf16[128,3,1,64]{3,2,1,0:T(2,128)(2,1)S(1)} fusion(bf16[2,128,3,128,64]{3,4,2,1,0:T(8,128)(2,1)} %param.32, bf16[128,3,128,1]{2,0,1,3:T(8,128)(2,1)} %fusion.39), kind=kOutput, calls=%fused_computation.13 | convolution fusion | flops 6291456 | bytes 6438912 | tf_op jit(solution)/shard_map/ths,thsd->thd/dot_general | solution.py:51
  99.9 0.7 copy.71
  100.7 1.9 convolution_convert_fusion.5
  102.6 34.6 %all-reduce.9.cloned.1.call-done = bf16[128,768]{1,0:T(8,128)(2,1)} async-done(((bf16[128,768]{1,0:T(8,128)(2,1)}), bf16[128,768]{1,0:T(8,128)(2,1)}) %all-reduce.9.cloned.1.call-update) | async-done | bytes 196624 | tf_op jit(solution)/shard_map/psum | solution.py:94
  137.3 1.1 fusion.61
  138.4 2.4 fusion.140
  140.8 3.1 convolution_convert_fusion.4
  143.9 0.2 all-reduce.13.cloned.1.call-start
  144.1 34.5 %all-reduce.11.cloned.1.call-done = bf16[128,768]{1,0:T(8,128)(2,1)} async-done(((bf16[128,768]{1,0:T(8,128)(2,1)}), bf16[128,768]{1,0:T(8,128)(2,1)}) %all-reduce.11.cloned.1.call-update) | async-done | bytes 196624 | tf_op jit(solution)/shard_map/psum | solution.py:98
  178.6 1.1 fusion.73
  179.7 1.3 convolution_convert_fusion.9
  181.0 1.3 convolution_convert_fusion.8
  182.3 1.3 convolution_convert_fusion.10
  183.7 2.1 multiply_reduce_fusion.1
  185.7 2.9 copy.78
  188.6 5.0 %fusion.25 = f32[128,3,32]{1,2,0:T(8,128)} fusion(f32[128,3,32]{1,2,0:T(8,128)} %copy.78, f32[128,32,3]{2,1,0:T(8,128)} %bitcast.193, pred[128,32]{1,0:T(8,128)(4,1)S(1)} %copy-done.18, pred[128,32]{1,0:T(8,128)(4,1)S(1)} %copy-done.16), kind=kOutput, calls=%fused_computation.46 | output fusion | flops 86846 | bytes 155648 | tf_op jit(solution)/shard_map/div | solution.py:38
  193.7 2.7 copy.91
  196.3 1.9 multiply_reduce_fusion
  198.3 0.9 convolution_convert_fusion.3
  199.4 0.2 reduce_window_sum.11
  199.6 0.6 select_reduce_fusion
  200.2 33.8 %all-reduce.13.cloned.1.call-done = bf16[128,768]{1,0:T(8,128)(2,1)} async-done(((bf16[128,768]{1,0:T(8,128)(2,1)}), bf16[128,768]{1,0:T(8,128)(2,1)}) %all-reduce.13.cloned.1.call-update) | async-done | bytes 196624 | tf_op jit(solution)/shard_map/psum | solution.py:89
  233.9 1.1 fusion.77
  235.0 1.4 convolution_convert_fusion.7
  236.6 4.5 %fusion.10 = f32[128,3,1,128]{3,2,1,0:T(1,128)S(1)} fusion(bf16[128,3,64,1]{2,3,1,0:T(2,128)(2,1)S(1)} %copy.84, bf16[2,128,3,128,64]{3,4,2,1,0:T(8,128)(2,1)} %param.31), kind=kOutput, calls=%fused_computation.11 | convolution fusion | flops 6291456 | bytes 6537216 | tf_op jit(solution)/shard_map/thd,thsd->ths/dot_general | solution.py:48
  241.1 1.6 fusion.40
  242.7 6.2 %fusion.8 = bf16[128,3,1,64]{3,2,1,0:T(2,128)(2,1)S(1)} fusion(bf16[2,128,3,128,64]{3,4,2,1,0:T(8,128)(2,1)} %param.32, bf16[128,3,128,1]{2,0,1,3:T(8,128)(2,1)} %fusion.40), kind=kOutput, calls=%fused_computation.9 | convolution fusion | flops 6291456 | bytes 6438912 | tf_op jit(solution)/shard_map/ths,thsd->thd/dot_general | solution.py:51
  248.9 0.7 copy.87
  249.7 1.7 convolution_convert_fusion.2
  251.4 0.7 fusion.145
  252.1 34.0 %all-reduce.15.cloned.1.call-done = bf16[128,768]{1,0:T(8,128)(2,1)} async-done(((bf16[128,768]{1,0:T(8,128)(2,1)}), bf16[128,768]{1,0:T(8,128)(2,1)}) %all-reduce.15.cloned.1.call-update) | async-done | bytes 196624 | tf_op jit(solution)/shard_map/psum | solution.py:94
  286.1 1.1 fusion.81
  287.2 0.3 convolution_convert_fusion
  287.5 10.0 %all_to_all.36 = bf16[8,32,768]{2,1,0:T(8,128)(2,1)S(1)} all-to-all(bf16[8,32,768]{2,1,0:T(8,128)(2,1)S(1)} %convolution_convert_fusion), channel_id=1, replica_groups=mesh['dp'=2,'tp'=4,'ep'=4] {'ep'}, dimensions={0} | all-to-all | bytes 786432 | tf_op jit(solution)/shard_map/all_to_all | solution.py:71
  297.5 1.4 fusion.184
  298.9 4.4 %convolution_convert_fusion.1 = bf16[2,128,768]{2,1,0:T(8,128)(2,1)} fusion(bf16[2,768,768]{2,1,0:T(8,128)(2,1)} %param.47, bf16[2,128,768]{2,1,0:T(8,128)(2,1)S(1)} %bitcast.173, bf16[2,768,768]{2,1,0:T(8,128)(2,1)} %param.46, f32[2,128,768]{2,1,0:T(8,128)} %fusion.184), kind=kOutput, calls=%fused_computation.50 | convolution fusion | flops 606142464 | bytes 6291456 | tf_op jit(solution)/shard_map/ecf,efd->ecd/dot_general | solution.py:75
  303.4 3.2 broadcast_select_fusion.1
  306.6 3.0 pad_maximum_fusion
  309.6 29.7 %all-reduce.17.cloned.1.call-done = bf16[2,128,768]{2,1,0:T(8,128)(2,1)} async-done(((bf16[2,128,768]{2,1,0:T(8,128)(2,1)}), bf16[2,128,768]{2,1,0:T(8,128)(2,1)}) %all-reduce.17.cloned.1.call-update) | async-done | bytes 393232 | tf_op jit(solution)/shard_map/psum | solution.py:76
  339.4 2.1 copy.53
  341.5 3.5 all-to-all-start.1
  345.0 0.2 fusion.179
  345.3 6.8 %all-to-all-done.1 = bf16[2,128,768]{2,0,1:T(2,128)(2,1)S(1)} async-done(((bf16[2,128,768]{2,0,1:T(2,128)(2,1)}), bf16[2,128,768]{2,0,1:T(2,128)(2,1)S(1)}, u32[]{:S(2)}, u32[]{:S(2)}) %all-to-all-start.1) | async-done | bytes 393248 | tf_op jit(solution)/shard_map/all_to_all | solution.py:77
  352.2 0.9 fusion.33
  (78 shorter events, 1.3 us)
Async XLA Ops:
  7.2 290.4 %copy-start = (bf16[2,768,768]{2,1,0:T(8,128)(2,1)S(1)}, bf16[2,768,768]{2,1,0:T(8,128)(2,1)}, u32[]{:S(2)}) copy-start(bf16[2,768,768]{2,1,0:T(8,128)(2,1)} %param.45) | copy-start | bytes 7077892
  7.2 76.9 %all-reduce.7.cloned.1.call-start = ((), (), s32[]{:S(2)}) async-start(), calls=%async_computation.2 | async-start | bytes 393216 | tf_op jit(solution)/shard_map/psum | solution.py:89
  8.1 27.6 %copy-start.15 = (pred[128,32]{1,0:T(8,128)(4,1)}, pred[128,32]{1,0:T(8,128)(4,1)S(1)}, u32[]{:S(2)}) copy-start(pred[128,32]{1,0:T(8,128)(4,1)S(1)} %get-tuple-element.22) | copy-start | bytes 12292
  8.1 27.6 %copy-start.17 = (pred[128,32]{1,0:T(8,128)(4,1)}, pred[128,32]{1,0:T(8,128)(4,1)S(1)}, u32[]{:S(2)}) copy-start(pred[128,32]{1,0:T(8,128)(4,1)S(1)} %get-tuple-element.23) | copy-start | bytes 12292
  13.5 8.0 %copy-start.6 = (bf16[128,192]{0,1:T(8,128)(2,1)}, bf16[128,192]{0,1:T(8,128)(2,1)S(1)}, u32[]{:S(2)}) copy-start(bf16[128,192]{0,1:T(8,128)(2,1)S(1)} %convolution_convert_fusion.13) | copy-start | bytes 147460
  14.9 28.6 %copy-start.10 = (bf16[128,192]{0,1:T(8,128)(2,1)}, bf16[128,192]{0,1:T(8,128)(2,1)S(1)}, u32[]{:S(2)}) copy-start(bf16[128,192]{0,1:T(8,128)(2,1)S(1)} %convolution_convert_fusion.12) | copy-start | bytes 147460
  40.8 4.7 %copy-start.4 = (bf16[2,192,768]{2,1,0:T(8,128)(2,1)S(1)}, bf16[2,192,768]{2,1,0:T(8,128)(2,1)}, u32[]{:S(2)}) copy-start(bf16[2,192,768]{2,1,0:T(8,128)(2,1)} %param.38) | copy-start | bytes 1769476
  40.8 5.7 %copy-start.14 = (s32[128,128]{1,0:T(8,128)S(1)}, s32[128,128]{1,0:T(8,128)}, u32[]{:S(2)}) copy-start(s32[128,128]{1,0:T(8,128)} %param.27) | copy-start | bytes 196612
  40.8 43.3 %copy-start.1 = (bf16[128,768]{1,0:T(8,128)(2,1)S(1)}, bf16[128,768]{1,0:T(8,128)(2,1)}, u32[]{:S(2)}) copy-start(bf16[128,768]{1,0:T(8,128)(2,1)} %param.25) | copy-start | bytes 589828
  46.4 90.9 %all-reduce.9.cloned.1.call-start = ((), (), s32[]{:S(2)}) async-start(), calls=%async_computation.3 | async-start | bytes 393216 | tf_op jit(solution)/shard_map/psum | solution.py:94
  46.5 45.5 %copy-start.19 = (pred[128,128]{1,0:T(8,128)(4,1)}, pred[128,128]{1,0:T(8,128)(4,1)S(1)}, u32[]{:S(2)}) copy-start(pred[128,128]{1,0:T(8,128)(4,1)S(1)} %broadcast_compare_fusion.1) | copy-start | bytes 49156
  93.7 43.6 %copy-start.3 = (bf16[128,768]{1,0:T(8,128)(2,1)S(1)}, bf16[128,768]{1,0:T(8,128)(2,1)}, u32[]{:S(2)}) copy-start(bf16[128,768]{1,0:T(8,128)(2,1)} %all-reduce.7.cloned.1.call-done) | copy-start | bytes 589828
  102.6 76.0 %all-reduce.11.cloned.1.call-start = ((), (), s32[]{:S(2)}) async-start(), calls=%async_computation.4 | async-start | bytes 393216 | tf_op jit(solution)/shard_map/psum | solution.py:98
  143.9 90.0 %all-reduce.13.cloned.1.call-start = ((), (), s32[]{:S(2)}) async-start(), calls=%async_computation.5 | async-start | bytes 393216 | tf_op jit(solution)/shard_map/psum | solution.py:89
  181.0 7.6 %copy-start.8 = (bf16[128,192]{0,1:T(8,128)(2,1)}, bf16[128,192]{0,1:T(8,128)(2,1)S(1)}, u32[]{:S(2)}) copy-start(bf16[128,192]{0,1:T(8,128)(2,1)S(1)} %convolution_convert_fusion.9) | copy-start | bytes 147460
  182.3 14.0 %copy-start.12 = (bf16[128,192]{0,1:T(8,128)(2,1)}, bf16[128,192]{0,1:T(8,128)(2,1)S(1)}, u32[]{:S(2)}) copy-start(bf16[128,192]{0,1:T(8,128)(2,1)S(1)} %convolution_convert_fusion.8) | copy-start | bytes 147460
  183.6 5.0 %copy-start.16 = (pred[128,32]{1,0:T(8,128)(4,1)S(1)}, pred[128,32]{1,0:T(8,128)(4,1)}, u32[]{:S(2)}) copy-start(pred[128,32]{1,0:T(8,128)(4,1)} %copy-done.15) | copy-start | bytes 12292
  183.6 5.0 %copy-start.18 = (pred[128,32]{1,0:T(8,128)(4,1)S(1)}, pred[128,32]{1,0:T(8,128)(4,1)}, u32[]{:S(2)}) copy-start(pred[128,32]{1,0:T(8,128)(4,1)} %copy-done.17) | copy-start | bytes 12292
  193.7 5.6 %copy-start.20 = (s32[128]{0:T(128)S(1)}, s32[128]{0:T(128)}, u32[]{:S(2)}) copy-start(s32[128]{0:T(128)} %param.28) | copy-start | bytes 1540
  196.3 38.7 %copy-start.21 = (f32[768]{0:T(1024)S(1)}, f32[768]{0:T(1024)}, u32[]{:S(2)}) copy-start(f32[768]{0:T(1024)} %get-tuple-element.9) | copy-start | bytes 9220
  199.2 86.9 %all-reduce.15.cloned.1.call-start = ((), (), s32[]{:S(2)}) async-start(), calls=%async_computation.6 | async-start | bytes 393216 | tf_op jit(solution)/shard_map/psum | solution.py:94
  242.7 7.0 %copy-start.5 = (bf16[2,192,768]{2,1,0:T(8,128)(2,1)S(1)}, bf16[2,192,768]{2,1,0:T(8,128)(2,1)}, u32[]{:S(2)}) copy-start(bf16[2,192,768]{2,1,0:T(8,128)(2,1)} %param.40) | copy-start | bytes 1769476
  242.7 43.4 %copy-start.2 = (bf16[128,768]{1,0:T(8,128)(2,1)S(1)}, bf16[128,768]{1,0:T(8,128)(2,1)}, u32[]{:S(2)}) copy-start(bf16[128,768]{1,0:T(8,128)(2,1)} %all-reduce.13.cloned.1.call-done) | copy-start | bytes 589828
  251.4 88.0 %all-reduce.17.cloned.1.call-start = ((), (), s32[]{:S(2)}) async-start(), calls=%async_computation.7 | async-start | bytes 786432 | tf_op jit(solution)/shard_map/psum | solution.py:76
  298.9 4.5 %copy-start.7 = (bf16[128,192]{0,1:T(8,128)(2,1)S(1)}, bf16[128,192]{0,1:T(8,128)(2,1)}, u32[]{:S(2)}) copy-start(bf16[128,192]{0,1:T(8,128)(2,1)} %copy-done.6) | copy-start | bytes 147460
  298.9 4.5 %copy-start.9 = (bf16[128,192]{0,1:T(8,128)(2,1)S(1)}, bf16[128,192]{0,1:T(8,128)(2,1)}, u32[]{:S(2)}) copy-start(bf16[128,192]{0,1:T(8,128)(2,1)} %copy-done.8) | copy-start | bytes 147460
  298.9 4.5 %copy-start.11 = (bf16[128,192]{0,1:T(8,128)(2,1)S(1)}, bf16[128,192]{0,1:T(8,128)(2,1)}, u32[]{:S(2)}) copy-start(bf16[128,192]{0,1:T(8,128)(2,1)} %copy-done.10) | copy-start | bytes 147460
  298.9 4.5 %copy-start.13 = (bf16[128,192]{0,1:T(8,128)(2,1)S(1)}, bf16[128,192]{0,1:T(8,128)(2,1)}, u32[]{:S(2)}) copy-start(bf16[128,192]{0,1:T(8,128)(2,1)} %copy-done.12) | copy-start | bytes 147460
  306.6 38.3 %copy-start.22 = (f32[768,8]{0,1:T(8,128)S(1)}, f32[768,8]{0,1:T(8,128)}, u32[]{:S(2)}) copy-start(f32[768,8]{0,1:T(8,128)} %param.44) | copy-start | bytes 73732
  341.5 10.6 %all-to-all-start.1 = ((bf16[2,128,768]{2,0,1:T(2,128)(2,1)}), bf16[2,128,768]{2,0,1:T(2,128)(2,1)S(1)}, u32[]{:S(2)}, u32[]{:S(2)}) async-start(bf16[2,128,768]{2,0,1:T(2,128)(2,1)} %copy.53), calls=%async_computation.1 | async-start | bytes 786432 | tf_op jit(solution)/shard_map/all_to_all | solution.py:77
Sparse Core Ops, SparseCore 0:
  46.5 37.5 all-reduce.6
  102.7 34.5 all-reduce.8
  144.0 34.5 all-reduce.10
  199.3 34.5 all-reduce.12
  251.5 34.5 all-reduce.14
  303.5 35.8 all-reduce.16
where the time goes:
time: 361 us; the launch traced here: 360 us
  waiting for transfers between devices  211 us (58%)
  matrix products  51.1 us (14%)
  other arithmetic  37.4 us (10%)
  local copies, waits for them, and re-layouts  31.9 us (9%)
  between operations  14.5 us (4%)
  blocking collectives  9.95 us (3%)
  starting transfers between devices  3.89 us (1%)
    psum x2, waiting for transfers between devices, decode_body(): h_cur = add_residual(h_cur, lax.psum(attn_part.astype(jnp.bfloat16), 'tp'))  71.4 us
    psum x2, waiting for transfers between devices, decode_body(): h_cur = add_residual(h_cur, lax.psum(cross_part.astype(jnp.bfloat16), 'tp'))  68.6 us
    psum x1, waiting for transfers between devices, decode_body(): h_cur = add_residual(h_cur, lax.psum(ffn_part.astype(jnp.bfloat16), 'tp'))  34.5 us
    psum x1, waiting for transfers between devices, switch_layer(): expert_out = lax.psum(expert_out, 'tp')  29.7 us
    dot_general x14, matrix products, project(): return jnp.dot(normed, weight, preferred_element_type=jnp.float32)  21.7 us
    gather x1, local copies, waits for them, and re-layouts, self_attention(): bias = jnp.take(rel_bias, jnp.maximum(distance, 0), axis=1)  14.2 us
    dot_general x2, matrix products, cross_attention(): jnp.einsum('ths,thsd->thd', attn_prob, values, preferred_element_type=jnp...  12.5 us
    div x2, other arithmetic, self_attention(): attn_prob = jax.nn.softmax(scores, axis=-1).astype(jnp.bfloat16)  10.1 us
  transfers between devices with their start and end apart: 7, of which 7 were waited for; matrix products, arithmetic and copies ran while one was open for 2% of the time, Pallas kernels for 0%

commit v1 on v0

v1 whole, which is shorter than its diff:
```python
import functools

import jax
import jax.numpy as jnp
from jax import lax
from jax.experimental import pallas as pl
from jax.experimental.pallas import tpu as pltpu
from jax.sharding import PartitionSpec as P

EPS = 1e-6
NEG_BIG = -1e9
F32 = jnp.float32
BF16 = jnp.bfloat16
MESH = pl.DeviceIdType.MESH

TOK = 128
D = 768
WID = 192
HEADS = 3
HEAD = 64
CACHE = 32
SRC = 128
ROWS = 32
EXP = 8
CAP = 32


def xor_peer(me, m):
    flip1 = me + 1 - 2 * lax.rem(me, 2)
    if m == 1:
        return flip1
    if m == 2:
        return lax.rem(me + 2, 4)
    return 3 - me


def rms(h_float, scale):
    inv_rms = lax.rsqrt(jnp.mean(h_float * h_float, axis=-1, keepdims=True) + EPS)
    return (h_float * inv_rms * scale).astype(BF16)


def dot(a, b, dims):
    return lax.dot_general(a, b, (dims, ((), ())), preferred_element_type=F32)


NN = ((1,), (0,))
NT = ((1,), (1,))


def kernel(bias_ref, hid_ref, pos_ref, exp_ref, mask_ref, scale_ref, router_ref,
           kc, vc, ck, cv, wq, wk, wv, wo, wcq, wco, wdg, wdu, wdd, weg, weu, wed,
           h_out, kc_out, vc_out,
           kb, vb, ckb, cvb, wqkv, wob, wcqb, wcob, dgb, dub, ddb, egb, eub, edb,
           biasb, sb, q32, ctxb, hown, part, rsb, xb, disp, dispt, recv, eout, ret, gatec,
           in_sem, out_sem, rs_s, rs_r, ag_s, ag_r, a_s, a_r, b_s, b_r):
    me = lax.axis_index("tp")
    ep = lax.axis_index("ep")
    barrier = pltpu.get_barrier_semaphore()
    for m in (1, 2, 3):
        pl.semaphore_signal(barrier, inc=1, device_id={"tp": xor_peer(me, m)}, device_id_type=MESH)
        pl.semaphore_signal(barrier, inc=1, device_id={"ep": xor_peer(ep, m)}, device_id_type=MESH)

    loads = {}

    def load(key, src, dst):
        copy = pltpu.make_async_copy(src, dst, in_sem.at[len(loads)])
        copy.start()
        loads[key] = copy

    def need(*keys):
        for key in keys:
            loads[key].wait()

    def load_self(layer):
        load(f"q{layer}", wq.at[layer], wqkv.at[layer, pl.ds(0, WID)])
        load(f"k{layer}", wk.at[layer], wqkv.at[layer, pl.ds(WID, WID)])
        load(f"v{layer}", wv.at[layer], wqkv.at[layer, pl.ds(2 * WID, WID)])
        load(f"kc{layer}", kc.at[layer], kb.at[layer])
        load(f"vc{layer}", vc.at[layer], vb.at[layer])
        load(f"o{layer}", wo.at[layer], wob.at[layer])

    def load_cross(layer):
        load(f"cq{layer}", wcq.at[layer], wcqb.at[layer])
        load(f"ck{layer}", ck.at[layer], ckb.at[layer])
        load(f"cv{layer}", cv.at[layer], cvb.at[layer])
        load(f"co{layer}", wco.at[layer], wcob.at[layer])

    load_self(0)

    sends = []

    def rs_start(ph, value):
        part[ph] = value.astype(BF16)
        copies = []
        for m in (3, 2, 1):
            peer = xor_peer(me, m)
            copy = pltpu.make_async_remote_copy(
                src_ref=part.at[ph, pl.ds(pl.multiple_of(peer * ROWS, ROWS), ROWS)],
                dst_ref=rsb.at[ph, m - 1],
                send_sem=rs_s.at[ph, m - 1], recv_sem=rs_r.at[ph, m - 1],
                device_id={"tp": peer}, device_id_type=MESH)
            copy.start()
            copies.append(copy)
        sends.extend(copies)
        return copies

    def rs_finish(ph, copies):
        total = part[ph, pl.ds(pl.multiple_of(me * ROWS, ROWS), ROWS), :].astype(F32)
        for copy, m in zip(copies[::-1], (1, 2, 3)):
            copy.wait_recv()
            total = total + rsb[ph, m - 1].astype(F32)
        return total.astype(BF16).astype(F32)

    def gather(ph, own):
        mine = pl.ds(pl.multiple_of(me * ROWS, ROWS), ROWS)
        xb[ph, mine, :] = own
        copies = []
        for m in (3, 2, 1):
            copy = pltpu.make_async_remote_copy(
                src_ref=xb.at[ph, mine], dst_ref=xb.at[ph, mine],
                send_sem=ag_s.at[ph, m - 1], recv_sem=ag_r.at[ph, m - 1],
                device_id={"tp": xor_peer(me, m)}, device_id_type=MESH)
            copy.start()
            copies.append(copy)
        sends.extend(copies)
        for copy in copies[::-1]:
            copy.wait_recv()
        return xb[ph]

    def add_own(delta):
        new = (hown[...] + delta).astype(BF16).astype(F32)
        hown[...] = new
        return new

    pos = pos_ref[...]
    slot_id = lax.broadcasted_iota(jnp.int32, (CACHE, TOK), 0)
    dist = pos - slot_id
    for h in range(HEADS):
        acc = jnp.full((CACHE, TOK), NEG_BIG, F32)
        for d in range(CACHE):
            acc = jnp.where(dist == d, bias_ref[h, d], acc)
        biasb[h] = acc

    def self_attn(layer, x):
        need(f"q{layer}", f"k{layer}", f"v{layer}")
        qkv = dot(wqkv[layer], x, NT).astype(BF16).astype(F32)
        at_slot = dist == 0
        valid = dist >= 0
        need(f"kc{layer}")
        probs = []
        for h in range(HEADS):
            q = qkv[h * HEAD:(h + 1) * HEAD]
            k_new = qkv[WID + h * HEAD:WID + (h + 1) * HEAD]
            for g in range(CACHE // 8):
                kf = kb[layer, h, g * 8:(g + 1) * 8].astype(F32)
                sb[h, g * 8:(g + 1) * 8] = jnp.sum(kf * q[None], axis=1)
            s_new = jnp.sum(q * k_new, axis=0, keepdims=True)
            s = jnp.where(at_slot, s_new, sb[h])
            s = jnp.where(valid, s + biasb[h], NEG_BIG)
            e = jnp.exp(s - jnp.max(s, axis=0, keepdims=True))
            p = e / jnp.sum(e, axis=0, keepdims=True)
            probs.append(p.astype(BF16).astype(F32))
        need(f"vc{layer}")
        outs = []
        for h in range(HEADS):
            v_new = qkv[2 * WID + h * HEAD:2 * WID + (h + 1) * HEAD]
            p_new = jnp.sum(jnp.where(at_slot, probs[h], 0.0), axis=0, keepdims=True)
            sb[h] = jnp.where(at_slot, 0.0, probs[h])
            acc = p_new * v_new
            for j in range(CACHE):
                acc = acc + sb[h, j:j + 1] * vb[layer, h, j].astype(F32)
            outs.append(acc)
        ctx = jnp.concatenate(outs, axis=0).T.astype(BF16)
        need(f"o{layer}")
        return dot(ctx, wob[layer], NN), qkv

    def update_cache(layer, qkv):
        for buf, out, base, key in ((kb, kc_out, WID, 0), (vb, vc_out, 2 * WID, 1)):
            for h in range(HEADS):
                new = qkv[base + h * HEAD:base + (h + 1) * HEAD]
                for j in range(CACHE):
                    buf[layer, h, j] = jnp.where(pos == j, new, buf[layer, h, j].astype(F32)).astype(BF16)
            pltpu.make_async_copy(buf.at[layer], out.at[layer], out_sem.at[layer, key]).start()

    head_row = lax.broadcasted_iota(jnp.int32, (8, WID), 0)
    head_col = lax.broadcasted_iota(jnp.int32, (8, WID), 1)
    low = head_row * HEAD
    head_mask = jnp.where((head_col >= low) & (head_col < low + HEAD), 1.0, 0.0)
    GRP = 16

    def cross_attn(layer, x):
        need(f"cq{layer}")
        q32[...] = dot(x, wcqb[layer], NT).astype(BF16).astype(F32)
        need(f"ck{layer}", f"cv{layer}")

        def group(g, carry):
            base = pl.multiple_of(g * GRP, GRP)
            scores = []
            rows = []
            q_grp = q32[pl.ds(base, GRP), :]
            m_grp = mask_ref[pl.ds(base, GRP), :]
            for i in range(GRP):
                qrow = jnp.broadcast_to(q_grp[i:i + 1], (8, WID))
                qbd = (qrow * head_mask).astype(BF16)
                s = dot(qbd, ckb[layer, base + i], NN)
                m = jnp.broadcast_to(m_grp[i:i + 1], (8, SRC))
                scores.append(jnp.where(m > 0, s, NEG_BIG))
            s = jnp.concatenate(scores, axis=0)
            e = jnp.exp(s - jnp.max(s, axis=-1, keepdims=True))
            p = e / jnp.sum(e, axis=-1, keepdims=True)
            for i in range(GRP):
                c = dot(p[i * 8:(i + 1) * 8].astype(BF16), cvb[layer, base + i], NT)
                rows.append(jnp.sum(c * head_mask, axis=0, keepdims=True))
            ctxb[pl.ds(base, GRP), :] = jnp.concatenate(rows, axis=0)
            return carry

        lax.fori_loop(0, TOK // GRP, group, 0)
        need(f"co{layer}")
        return dot(ctxb[...].astype(BF16), wcob[layer], NN)

    def glu(x, w_gate, w_up):
        return (jax.nn.gelu(dot(x, w_gate, NN)) * dot(x, w_up, NN)).astype(BF16)

    mine = pl.ds(pl.multiple_of(me * ROWS, ROWS), ROWS)
    hown[...] = hid_ref[mine, :].astype(F32)
    x = rms(hid_ref[...].astype(F32), scale_ref[0, 0:1, :])

    for layer in range(2):
        ph = 3 * layer
        partial, qkv = self_attn(layer, x)
        if layer == 0:
            pl.semaphore_wait(barrier, 6)
        copies = rs_start(ph, partial)
        if layer == 0:
            load_cross(0)
            load("dg", wdg, dgb)
            load("du", wdu, dub)
            load("dd", wdd, ddb)
            load_self(1)
            load_cross(1)
            load("eg", weg, egb)
            load("eu", weu, eub)
            load("ed", wed, edb)
        update_cache(layer, qkv)
        new = add_own(rs_finish(ph, copies))
        x = gather(ph, rms(new, scale_ref[1, layer:layer + 1, :]))
        copies = rs_start(ph + 1, cross_attn(layer, x))
        new = add_own(rs_finish(ph + 1, copies))
        x = gather(ph + 1, rms(new, scale_ref[2, layer:layer + 1, :]))
        if layer == 0:
            need("dg", "du", "dd")
            copies = rs_start(2, dot(glu(x, dgb[...], dub[...]), ddb[...], NN))
            new = add_own(rs_finish(2, copies))
            x = gather(2, rms(new, scale_ref[0, 1:2, :]))

    expert = exp_ref[...]
    onehot = jnp.where(lax.broadcasted_iota(jnp.int32, (EXP, TOK), 0) == expert, 1.0, 0.0)
    r_id = lax.broadcasted_iota(jnp.int32, (TOK, TOK), 0)
    c_id = lax.broadcasted_iota(jnp.int32, (TOK, TOK), 1)
    before = jnp.where(r_id < c_id, 1.0, 0.0).astype(BF16)
    count = dot(onehot.astype(BF16), before, NN)
    slot = jnp.sum(count * onehot, axis=0, keepdims=True)
    target = jnp.where(slot < CAP, expert.astype(F32) * CAP + slot, -1.0)
    place = jnp.where(lax.broadcasted_iota(jnp.int32, (EXP * CAP, TOK), 0).astype(F32) == target, 1.0, 0.0)
    disp[...] = dot(place.astype(BF16), x, NN).astype(BF16)

    two = 2 * CAP

    def ep_rows(e):
        return pl.ds(pl.multiple_of(e * two, two), two)

    copies = []
    for m in (3, 2, 1):
        peer = xor_peer(ep, m)
        copy = pltpu.make_async_remote_copy(
            src_ref=disp.at[ep_rows(peer)], dst_ref=recv.at[m],
            send_sem=a_s.at[m - 1], recv_sem=a_r.at[m - 1],
            device_id={"ep": peer}, device_id_type=MESH)
        copy.start()
        copies.append(copy)
    sends.extend(copies)
    recv[0] = disp[ep_rows(ep), :]
    dispt[...] = place.T.astype(BF16)

    logits = lax.dot_general(router_ref[...], x.astype(F32), (NT, ((), ())), precision=lax.Precision.HIGHEST,
                             preferred_element_type=F32)
    e = jnp.exp(logits - jnp.max(logits, axis=0, keepdims=True))
    route = e / jnp.sum(e, axis=0, keepdims=True)
    gate_row = jnp.sum(route * onehot, axis=0, keepdims=True)
    gatec[...] = jnp.broadcast_to(gate_row, (TOK, TOK)).T

    need("eg", "eu", "ed")
    for copy in copies:
        copy.wait_recv()
    for j in range(2):
        rows = recv[:, j * CAP:(j + 1) * CAP, :].reshape(4 * CAP, D)
        out = dot(glu(rows, egb[j], eub[j]), edb[j], NN).astype(BF16)
        eout[:, j * CAP:(j + 1) * CAP, :] = out.reshape(4, CAP, D)
    copies = []
    for m in (3, 2, 1):
        peer = xor_peer(ep, m)
        copy = pltpu.make_async_remote_copy(
            src_ref=eout.at[m], dst_ref=ret.at[ep_rows(ep)],
            send_sem=b_s.at[m - 1], recv_sem=b_r.at[m - 1],
            device_id={"ep": peer}, device_id_type=MESH)
        copy.start()
        copies.append(copy)
    sends.extend(copies)
    ret[ep_rows(ep), :] = eout[0]
    for copy in copies:
        copy.wait_recv()
    copies = rs_start(5, dot(dispt[...], ret[...], NN))
    y = rs_finish(5, copies)
    gate_own = gatec[mine, :][:, 0:1]
    new = (hown[...] + gate_own * y).astype(BF16)
    h_out[...] = gather(5, new)

    for copy in sends:
        copy.wait_send()
    for layer in range(2):
        pltpu.make_async_copy(kb.at[layer], kc_out.at[layer], out_sem.at[layer, 0]).wait()
        pltpu.make_async_copy(vb.at[layer], vc_out.at[layer], out_sem.at[layer, 1]).wait()


def decode_body(hidden, write_pos, enc_mask, expert_idx, self_keys, self_values, cross_keys, cross_values, rel_bias, norm_scale, w_query, w_key, w_value, w_out, w_cross_query, w_cross_out, dense_gate, dense_up, dense_down, router, exp_gate, exp_up, exp_down):
    k_t = jnp.transpose(self_keys, (0, 2, 3, 4, 1))
    v_t = jnp.transpose(self_values, (0, 2, 3, 4, 1))
    ck_t = jnp.transpose(cross_keys, (0, 1, 2, 4, 3)).reshape(2, TOK, WID, SRC)
    cv_t = jnp.transpose(cross_values, (0, 1, 2, 4, 3)).reshape(2, TOK, WID, SRC)
    swap = lambda w: jnp.transpose(w, (0, 2, 1))
    vmem = pl.BlockSpec(memory_space=pltpu.VMEM)
    hbm = pl.BlockSpec(memory_space=pl.ANY)
    smem = pl.BlockSpec(memory_space=pltpu.SMEM)
    cache = (2, HEADS, CACHE, HEAD, TOK)
    dma = pltpu.SemaphoreType.DMA
    h_new, k_new, v_new = pl.pallas_call(
        kernel,
        out_shape=(jax.ShapeDtypeStruct((TOK, D), BF16), jax.ShapeDtypeStruct(cache, BF16), jax.ShapeDtypeStruct(cache, BF16)),
        in_specs=[smem] + [vmem] * 6 + [hbm] * 16,
        out_specs=(vmem, hbm, hbm),
        scratch_shapes=[
            pltpu.VMEM(cache, BF16), pltpu.VMEM(cache, BF16),
            pltpu.VMEM((2, TOK, WID, SRC), BF16), pltpu.VMEM((2, TOK, WID, SRC), BF16),
            pltpu.VMEM((2, 3 * WID, D), BF16), pltpu.VMEM((2, WID, D), BF16),
            pltpu.VMEM((2, WID, D), BF16), pltpu.VMEM((2, WID, D), BF16),
            pltpu.VMEM((D, D), BF16), pltpu.VMEM((D, D), BF16), pltpu.VMEM((D, D), BF16),
            pltpu.VMEM((2, D, D), BF16), pltpu.VMEM((2, D, D), BF16), pltpu.VMEM((2, D, D), BF16),
            pltpu.VMEM((HEADS, CACHE, TOK), F32), pltpu.VMEM((HEADS, CACHE, TOK), F32),
            pltpu.VMEM((TOK, WID), F32), pltpu.VMEM((TOK, WID), F32), pltpu.VMEM((ROWS, D), F32),
            pltpu.VMEM((6, TOK, D), BF16), pltpu.VMEM((6, 3, ROWS, D), BF16), pltpu.VMEM((6, TOK, D), BF16),
            pltpu.VMEM((EXP * CAP, D), BF16), pltpu.VMEM((TOK, EXP * CAP), BF16),
            pltpu.VMEM((4, 2 * CAP, D), BF16), pltpu.VMEM((4, 2 * CAP, D), BF16), pltpu.VMEM((EXP * CAP, D), BF16),
            pltpu.VMEM((TOK, TOK), F32),
            dma((32,)), dma((2, 2)), dma((6, 3)), dma((6, 3)), dma((6, 3)), dma((6, 3)),
            dma((3,)), dma((3,)), dma((3,)), dma((3,)),
        ],
        compiler_params=pltpu.CompilerParams(collective_id=0, has_side_effects=True, vmem_limit_bytes=63 << 20),
        name="decode",
    )(rel_bias, hidden, write_pos.reshape(1, TOK), expert_idx.reshape(1, TOK), enc_mask, jnp.transpose(norm_scale, (1, 0, 2)), router.T,
      k_t, v_t, ck_t, cv_t, swap(w_query), swap(w_key), swap(w_value), w_out, swap(w_cross_query), w_cross_out,
      dense_gate, dense_up, dense_down, exp_gate, exp_up, exp_down)
    back = lambda c: jnp.transpose(c, (0, 4, 1, 2, 3))
    return h_new, back(k_new), back(v_new)


def solution(mesh):
    batch = ('dp', 'ep')
    row_spec = P(batch, None)
    vec_spec = P(batch)
    cache_spec = P(None, batch, 'tp', None, None)
    col_spec = P(None, None, 'tp')
    out_rows = P(None, 'tp', None)
    in_specs = (row_spec, vec_spec, row_spec, vec_spec, cache_spec, cache_spec, cache_spec, cache_spec, P('tp', None), P(), col_spec, col_spec, col_spec, out_rows, col_spec, out_rows, P(None, 'tp'), P(None, 'tp'), P('tp', None), P(), P('ep', None, 'tp'), P('ep', None, 'tp'), P('ep', 'tp', None))
    out_specs = (row_spec, cache_spec, cache_spec)
    return jax.shard_map(decode_body, mesh=mesh, in_specs=in_specs, out_specs=out_specs, check_vma=False)
```

time: 361 us -> 113 us (0.31)
  waiting for transfers between devices: 211 us -> 0 us
  Pallas kernels: 0 us -> 104 us
  matrix products: 51.1 us -> 0 us
  other arithmetic: 37.4 us -> 0 us
  local copies, waits for them, and re-layouts: 31.9 us -> 8.14 us
  between operations: 14.5 us -> 0.65 us
  blocking collectives: 9.95 us -> 0 us
  starting transfers between devices: 3.89 us -> 0 us
    psum x6 -> x0, waiting for transfers between devices: 204 us -> none  [the longest x2 71.4 us: decode_body(): h_cur = add_residual(h_cur, lax.psum(attn_part.astype(jnp.bfloat16), 'tp'))]
    pallas_call x0 -> x1, Pallas kernels: none -> 104 us  [decode_body(): pl.pallas_call(kernel, out_shape=(jax.ShapeDtypeStruct((TOK, D), BF16), j...]
    dot_general x23 -> x0, matrix products: 51.1 us -> none  [the longest x14 21.7 us: project(): return jnp.dot(normed, weight, preferred_element_type=jnp.float32)]
    gather x1 -> x0, local copies, waits for them, and re-layouts: 14.2 us -> none  [self_attention(): bias = jnp.take(rel_bias, jnp.maximum(distance, 0), axis=1)]
    div x4 -> x0, other arithmetic: 13.5 us -> none  [the longest x2 10.1 us: self_attention(): attn_prob = jax.nn.softmax(scores, axis=-1).astype(jnp.bfloat16)]
    all_to_all x1 -> x0, blocking collectives: 9.95 us -> none  [switch_layer(): received = lax.all_to_all(buffers, 'ep', 0, 1, tiled=True)]
    dot_general x4 -> x0, local copies, waits for them, and re-layouts: 7.22 us -> none  [the longest x2 5.73 us: self_attention(): jnp.einsum('thd,thld->thl', query, keys, preferred_element_type=jnp.float32)]
    reduce_sum x9 -> x0, other arithmetic: 7.13 us -> none  [the longest x6 6.48 us: rms_norm(): jnp.mean(h_float * h_float, axis=-1, keepdims=True) + EPS]
  transfers between devices with their start and end apart: 7 -> 0, of which waited for: 7 -> 0; matrix products, arithmetic and copies ran while one was open for 2% -> 0% of each run, Pallas kernels for 0% -> 0%
where the time goes in v1:
time: 113 us
  Pallas kernels  104 us (92%)
  local copies, waits for them, and re-layouts  8.14 us (7%)
    pallas_call x1, Pallas kernels, decode_body(): pl.pallas_call(kernel, out_shape=(jax.ShapeDtypeStruct((TOK, D), BF16), j...  104 us
    unnamed x5, local copies, waits for them, and re-layouts  8.14 us

profile of v1, /device:TPU:0, one launch (start us, length us, event | category | flops | bytes accessed | tf_op | source)
XLA Modules:
  0.0 112.9 jit_solution(1228187364694875883)
XLA Ops:
  0.6 104.1 %decode.1 = (bf16[128,768]{1,0:T(8,128)(2,1)}, bf16[2,3,32,64,128]{4,3,2,1,0:T(8,128)(2,1)}, bf16[2,3,32,64,128]{4,3,2,1,0:T(8,128)(2,1)}) custom-call(f32[3,32]{1,0:T(4,128)} %bias_ref.1, bf16[128,768]{1,0:T(8,128)(2,1)} %hid_ref.1, s32[1,128]{1,0:T(1,128)} %bitcast.30, s32[1,128]{1,0:T(1,128)} %bitcast.31, s32[128,128]{1,0:T(8,128)} %mask_ref.1, ...), custom_call_target="tpu_custom_call" | custom-call | tf_op jit(solution)/shard_map/decode/pallas_call | solution.py:336
  104.7 1.6 %copy.29 = bf16[128,768]{1,0:T(8,128)(2,1)} copy(bf16[128,768]{1,0:T(8,128)(2,1)} %get-tuple-element.12) | data formatting | bytes 393216
  106.3 0.0 copy-start
  106.3 4.9 %copy.30 = bf16[2,128,3,32,64]{1,4,3,2,0:T(8,128)(2,1)} copy(bf16[2,128,3,32,64]{1,4,3,2,0:T(8,128)(2,1)} %bitcast.23) | data formatting | bytes 6291456
  111.2 0.0 copy-done
  111.2 1.7 %copy.31 = bf16[2,128,3,32,64]{1,4,3,2,0:T(8,128)(2,1)} copy(bf16[2,128,3,32,64]{1,4,3,2,0:T(8,128)(2,1)S(1)} %bitcast.22) | data formatting | bytes 6291456
Async XLA Ops:
  106.3 4.9 %copy-start = (bf16[2,3,32,64,128]{4,3,2,1,0:T(8,128)(2,1)S(1)}, bf16[2,3,32,64,128]{4,3,2,1,0:T(8,128)(2,1)}, u32[]{:S(2)}) copy-start(bf16[2,3,32,64,128]{4,3,2,1,0:T(8,128)(2,1)} %get-tuple-element.8) | copy-start | bytes 9437188

commit v2 on v1

v2 whole, which is shorter than its diff:
```python
import functools

import jax
import jax.numpy as jnp
from jax import lax
from jax.experimental import pallas as pl
from jax.experimental.pallas import tpu as pltpu
from jax.sharding import PartitionSpec as P

EPS = 1e-6
NEG_BIG = -1e9
F32 = jnp.float32
BF16 = jnp.bfloat16
MESH = pl.DeviceIdType.MESH

TOK = 128
D = 768
WID = 192
HEADS = 3
HEAD = 64
CACHE = 32
SRC = 128
HALF = 64
ROWS = 16
GRP = 16
VMEM_LIMIT = 55 << 20
EXP = 8
CAP = 32


def xor_peer(me, m):
    flip1 = me + 1 - 2 * lax.rem(me, 2)
    if m == 1:
        return flip1
    if m == 2:
        return lax.rem(me + 2, 4)
    return 3 - me


def rms(h_float, scale):
    inv_rms = lax.rsqrt(jnp.mean(h_float * h_float, axis=-1, keepdims=True) + EPS)
    return (h_float * inv_rms * scale).astype(BF16)


def dot(a, b, dims):
    return lax.dot_general(a, b, (dims, ((), ())), preferred_element_type=F32)


NN = ((1,), (0,))
NT = ((1,), (1,))


def kernel(bias_h, hid_h, pos_h, exp_h, mask_h, scale_h, router_h,
           kc, vc, ck, cv, wq, wk, wv, wo, wcq, wco, wdg, wdu, wdd, weg, weu, wed,
           h_out, kb, vb,
           bias_ref, hid_ref, pos_ref, exp_ref, mask_ref, scale_ref, router_ref,
           ckb, cvb, wqkv, wob, wcqb, wcob, dgb, dub, ddb, egb, eub, edb,
           biasb, sb, sc, pb, ctxb, part, rsb, hb, disp, dispt, recv, eout, ret, gatec,
           in_sem, rs_s, rs_r, ag_s, ag_r, a_s, a_r, b_s, b_r):
    me = lax.axis_index("tp")
    ep = lax.axis_index("ep")
    barrier = pltpu.get_barrier_semaphore()
    for m in (1, 2, 3):
        pl.semaphore_signal(barrier, inc=1, device_id={"tp": xor_peer(me, m)}, device_id_type=MESH)
        pl.semaphore_signal(barrier, inc=1, device_id={"ep": xor_peer(ep, m)}, device_id_type=MESH)

    loads = {}

    def load(key, src, dst):
        copy = pltpu.make_async_copy(src, dst, in_sem.at[len(loads)])
        copy.start()
        loads[key] = copy

    def need(*keys):
        for key in keys:
            loads[key].wait()

    def load_self(layer):
        load(f"q{layer}", wq.at[layer], wqkv.at[layer, pl.ds(0, WID)])
        load(f"k{layer}", wk.at[layer], wqkv.at[layer, pl.ds(WID, WID)])
        load(f"v{layer}", wv.at[layer], wqkv.at[layer, pl.ds(2 * WID, WID)])
        load(f"kc{layer}", kc.at[layer], kb.at[layer])
        load(f"vc{layer}", vc.at[layer], vb.at[layer])
        load(f"o{layer}", wo.at[layer], wob.at[layer])

    def load_cross(layer):
        load(f"cq{layer}", wcq.at[layer], wcqb.at[layer])
        load(f"ck{layer}", ck.at[layer], ckb.at[layer])
        load(f"cv{layer}", cv.at[layer], cvb.at[layer])
        load(f"co{layer}", wco.at[layer], wcob.at[layer])

    load("hid", hid_h, hid_ref)
    load("scale", scale_h, scale_ref)
    load("pos", pos_h, pos_ref)
    load("bias", bias_h, bias_ref)
    load_self(0)
    load("exp", exp_h, exp_ref)
    load("mask", mask_h, mask_ref)
    load("router", router_h, router_ref)

    def load_rest():
        load_cross(0)
        load("dg", wdg, dgb)
        load("du", wdu, dub)
        load("dd", wdd, ddb)
        load_self(1)
        load_cross(1)
        load("eg", weg, egb)
        load("eu", weu, eub)
        load("ed", wed, edb)

    sends = []
    pending = {}

    def block(p, owner):
        return pl.ds(pl.multiple_of(p * HALF + owner * ROWS, ROWS), ROWS)

    def rs_start(ph, p, value):
        part[ph, p * HALF:(p + 1) * HALF] = value.astype(BF16)
        for m in (3, 2, 1):
            peer = xor_peer(me, m)
            copy = pltpu.make_async_remote_copy(
                src_ref=part.at[ph, block(p, peer)], dst_ref=rsb.at[ph, p, m - 1],
                send_sem=rs_s.at[ph, p, m - 1], recv_sem=rs_r.at[ph, p, m - 1],
                device_id={"tp": peer}, device_id_type=MESH)
            copy.start()
            sends.append(copy)
            pending[ph, p, m] = copy

    def rs_finish(ph, p):
        total = part[ph, block(p, me), :].astype(F32)
        for m in (1, 2, 3):
            pending[ph, p, m].wait_recv()
            total = total + rsb[ph, p, m - 1].astype(F32)
        return total.astype(BF16).astype(F32)

    def gather_start(ph, p, own):
        mine = block(p, me)
        hb[ph, mine, :] = own
        for m in (3, 2, 1):
            copy = pltpu.make_async_remote_copy(
                src_ref=hb.at[ph, mine], dst_ref=hb.at[ph, mine],
                send_sem=ag_s.at[ph, p, m - 1], recv_sem=ag_r.at[ph, p, m - 1],
                device_id={"tp": xor_peer(me, m)}, device_id_type=MESH)
            copy.start()
            sends.append(copy)
            pending["g", ph, p, m] = copy

    def gather_wait(ph, p):
        for m in (1, 2, 3):
            pending["g", ph, p, m].wait_recv()
        return hb[ph, p * HALF:(p + 1) * HALF]

    def reduce_gather(ph, before):
        for p in (0, 1):
            own = before[block(p, me), :].astype(F32)
            gather_start(ph, p, (own + rs_finish(ph, p)).astype(BF16))

    def self_attn(layer, x):
        need(f"q{layer}", f"k{layer}", f"v{layer}")
        pos = pos_ref[...]
        dist = pos - lax.broadcasted_iota(jnp.int32, (CACHE, TOK), 0)
        at_slot = dist == 0
        valid = dist >= 0
        qkv = dot(wqkv[layer], x, NT).astype(BF16).astype(F32)
        if layer == 0:
            need("bias")
            for h in range(HEADS):
                acc = jnp.full((CACHE, TOK), NEG_BIG, F32)
                for d in range(CACHE):
                    acc = jnp.where(dist == d, bias_ref[h, d], acc)
                biasb[h] = acc
        need(f"kc{layer}")
        probs = []
        for h in range(HEADS):
            q = qkv[h * HEAD:(h + 1) * HEAD]
            k_new = qkv[WID + h * HEAD:WID + (h + 1) * HEAD]
            for g in range(CACHE // 8):
                kf = kb[layer, h, g * 8:(g + 1) * 8].astype(F32)
                sb[h, g * 8:(g + 1) * 8] = jnp.sum(kf * q[None], axis=1)
            s_new = jnp.sum(q * k_new, axis=0, keepdims=True)
            s = jnp.where(at_slot, s_new, sb[h])
            s = jnp.where(valid, s + biasb[h], NEG_BIG)
            e = jnp.exp(s - jnp.max(s, axis=0, keepdims=True))
            p = e / jnp.sum(e, axis=0, keepdims=True)
            probs.append(p.astype(BF16).astype(F32))
        need(f"vc{layer}")
        if layer == 0:
            load_rest()
        outs = []
        for h in range(HEADS):
            v_new = qkv[2 * WID + h * HEAD:2 * WID + (h + 1) * HEAD]
            p_new = jnp.sum(jnp.where(at_slot, probs[h], 0.0), axis=0, keepdims=True)
            sb[h] = jnp.where(at_slot, 0.0, probs[h])
            acc = p_new * v_new
            for j in range(CACHE):
                acc = acc + sb[h, j:j + 1] * vb[layer, h, j].astype(F32)
            outs.append(acc)
        ctx = jnp.concatenate(outs, axis=0).T.astype(BF16)
        need(f"o{layer}")
        partial = dot(ctx, wob[layer], NN)
        if layer == 0:
            pl.semaphore_wait(barrier, 6)
        for p in (0, 1):
            rs_start(3 * layer, p, partial[p * HALF:(p + 1) * HALF])
        for buf, base in ((kb, WID), (vb, 2 * WID)):
            for h in range(HEADS):
                new = qkv[base + h * HEAD:base + (h + 1) * HEAD]
                for j in range(CACHE):
                    buf[layer, h, j] = jnp.where(pos == j, new, buf[layer, h, j].astype(F32)).astype(BF16)

    head_row = lax.broadcasted_iota(jnp.int32, (8, WID), 0)
    head_col = lax.broadcasted_iota(jnp.int32, (8, WID), 1)
    low = head_row * HEAD
    head_mask = jnp.where((head_col >= low) & (head_col < low + HEAD), 1.0, 0.0)
    lane = lax.broadcasted_iota(jnp.int32, (HEAD, GRP * 8), 1)

    def cross_attn(layer, p, x):
        q = dot(x, wcqb[layer], NT).astype(BF16).astype(F32)
        for i in range(HALF):
            t = p * HALF + i
            qbd = (jnp.broadcast_to(q[i:i + 1], (8, WID)) * head_mask).astype(BF16)
            s = dot(qbd, ckb[layer, t], NN)
            m = jnp.broadcast_to(mask_ref[t:t + 1, :], (8, SRC))
            sc[i * 8:(i + 1) * 8] = jnp.where(m > 0, s, NEG_BIG)
        for g in range(HALF // GRP):
            s = sc[g * GRP * 8:(g + 1) * GRP * 8]
            e = jnp.exp(s - jnp.max(s, axis=-1, keepdims=True))
            pb[g * GRP * 8:(g + 1) * GRP * 8] = (e / jnp.sum(e, axis=-1, keepdims=True)).astype(BF16)
        for g in range(HALF // GRP):
            prob = pb[g * GRP * 8:(g + 1) * GRP * 8]
            acc = [jnp.zeros((HEAD, GRP * 8), F32)] * HEADS
            for i in range(GRP):
                c = dot(cvb[layer, p * HALF + g * GRP + i], prob, NT)
                for h in range(HEADS):
                    acc[h] = jnp.where(lane == i * 8 + h, c[h * HEAD:(h + 1) * HEAD], acc[h])
            rows = jnp.concatenate(acc, axis=0).T
            ctxb[g * GRP:(g + 1) * GRP, :] = jnp.sum(rows.reshape(GRP, 8, WID), axis=1)
        return dot(ctxb[...].astype(BF16), wcob[layer], NN)

    def glu(x, w_gate, w_up):
        return (jax.nn.gelu(dot(x, w_gate, NN)) * dot(x, w_up, NN)).astype(BF16)

    need("hid", "scale", "pos")
    x = rms(hid_ref[...].astype(F32), scale_ref[0, 0:1, :])

    for layer in range(2):
        ph = 3 * layer
        self_attn(layer, x)
        reduce_gather(ph, hid_ref if layer == 0 else hb.at[2])
        need(f"cq{layer}", f"ck{layer}", f"cv{layer}", f"co{layer}")
        if layer == 0:
            need("mask")
        for p in (0, 1):
            x = rms(gather_wait(ph, p).astype(F32), scale_ref[1, layer:layer + 1, :])
            rs_start(ph + 1, p, cross_attn(layer, p, x))
        reduce_gather(ph + 1, hb.at[ph])
        if layer == 0:
            need("dg", "du", "dd")
            for p in (0, 1):
                x = rms(gather_wait(1, p).astype(F32), scale_ref[2, 0:1, :])
                rs_start(2, p, dot(glu(x, dgb[...], dub[...]), ddb[...], NN))
            reduce_gather(2, hb.at[1])
            x = jnp.concatenate([rms(gather_wait(2, p).astype(F32), scale_ref[0, 1:2, :]) for p in (0, 1)], axis=0)

    need("exp", "router")
    expert = exp_ref[...]
    onehot = jnp.where(lax.broadcasted_iota(jnp.int32, (EXP, TOK), 0) == expert, 1.0, 0.0)
    r_id = lax.broadcasted_iota(jnp.int32, (TOK, TOK), 0)
    c_id = lax.broadcasted_iota(jnp.int32, (TOK, TOK), 1)
    before = jnp.where(r_id < c_id, 1.0, 0.0).astype(BF16)
    count = dot(onehot.astype(BF16), before, NN)
    slot = jnp.sum(count * onehot, axis=0, keepdims=True)
    target = jnp.where(slot < CAP, expert.astype(F32) * CAP + slot, -1.0)
    place = jnp.where(lax.broadcasted_iota(jnp.int32, (EXP * CAP, TOK), 0).astype(F32) == target, 1.0, 0.0)
    dispt[...] = place.T.astype(BF16)
    x = jnp.concatenate([rms(gather_wait(4, p).astype(F32), scale_ref[2, 1:2, :]) for p in (0, 1)], axis=0)
    disp[...] = dot(place.astype(BF16), x, NN).astype(BF16)

    def ep_rows(e, j):
        return pl.ds(pl.multiple_of((2 * e + j) * CAP, CAP), CAP)

    for j in (0, 1):
        for m in (3, 2, 1):
            peer = xor_peer(ep, m)
            copy = pltpu.make_async_remote_copy(
                src_ref=disp.at[ep_rows(peer, j)], dst_ref=recv.at[j, m],
                send_sem=a_s.at[j, m - 1], recv_sem=a_r.at[j, m - 1],
                device_id={"ep": peer}, device_id_type=MESH)
            copy.start()
            sends.append(copy)
            pending["a", j, m] = copy
    for j in (0, 1):
        recv[j, 0] = disp[ep_rows(ep, j), :]

    logits = lax.dot_general(router_ref[...], x.astype(F32), (NT, ((), ())), precision=lax.Precision.HIGHEST,
                             preferred_element_type=F32)
    e = jnp.exp(logits - jnp.max(logits, axis=0, keepdims=True))
    route = e / jnp.sum(e, axis=0, keepdims=True)
    gate_row = jnp.sum(route * onehot, axis=0, keepdims=True)
    gatec[...] = jnp.broadcast_to(gate_row, (TOK, TOK)).T

    need("eg", "eu", "ed")
    for j in (0, 1):
        for m in (1, 2, 3):
            pending["a", j, m].wait_recv()
        rows = recv[j].reshape(4 * CAP, D)
        eout[j] = dot(glu(rows, egb[j], eub[j]), edb[j], NN).astype(BF16).reshape(4, CAP, D)
        for m in (3, 2, 1):
            peer = xor_peer(ep, m)
            copy = pltpu.make_async_remote_copy(
                src_ref=eout.at[j, m], dst_ref=ret.at[ep_rows(ep, j)],
                send_sem=b_s.at[j, m - 1], recv_sem=b_r.at[j, m - 1],
                device_id={"ep": peer}, device_id_type=MESH)
            copy.start()
            sends.append(copy)
            pending["b", j, m] = copy
        ret[ep_rows(ep, j), :] = eout[j, 0]
    for j in (0, 1):
        for m in (1, 2, 3):
            pending["b", j, m].wait_recv()
    for p in (0, 1):
        rs_start(5, p, dot(dispt[p * HALF:(p + 1) * HALF], ret[...], NN))
    for p in (0, 1):
        y = rs_finish(5, p)
        mine = block(p, me)
        gather_start(5, p, (hb[4, mine, :].astype(F32) + gatec[mine, :][:, 0:1] * y).astype(BF16))
    for p in (0, 1):
        h_out[p * HALF:(p + 1) * HALF] = gather_wait(5, p)
    for copy in sends:
        copy.wait_send()


def store(h_v, k_v, v_v, h_o, k_o, v_o, sem):
    copies = [pltpu.make_async_copy(src, dst, sem.at[i]) for i, (src, dst) in enumerate(((k_v, k_o), (v_v, v_o), (h_v, h_o)))]
    for copy in copies:
        copy.start()
    for copy in copies:
        copy.wait()


def decode_body(hidden, write_pos, enc_mask, expert_idx, self_keys, self_values, cross_keys, cross_values, rel_bias, norm_scale, w_query, w_key, w_value, w_out, w_cross_query, w_cross_out, dense_gate, dense_up, dense_down, router, exp_gate, exp_up, exp_down):
    k_t = jnp.transpose(self_keys, (0, 2, 3, 4, 1))
    v_t = jnp.transpose(self_values, (0, 2, 3, 4, 1))
    ck_t = jnp.transpose(cross_keys, (0, 1, 2, 4, 3)).reshape(2, TOK, WID, SRC)
    cv_t = jnp.transpose(cross_values, (0, 1, 2, 4, 3)).reshape(2, TOK, WID, SRC)
    swap = lambda w: jnp.transpose(w, (0, 2, 1))
    vmem = pl.BlockSpec(memory_space=pltpu.VMEM)
    hbm = pl.BlockSpec(memory_space=pl.ANY)
    cache = (2, HEADS, CACHE, HEAD, TOK)
    dma = pltpu.SemaphoreType.DMA
    out_shape = (jax.ShapeDtypeStruct((TOK, D), BF16), jax.ShapeDtypeStruct(cache, BF16), jax.ShapeDtypeStruct(cache, BF16))
    outs = pl.pallas_call(
        kernel,
        out_shape=tuple(pltpu.VMEM(o.shape, o.dtype) for o in out_shape),
        in_specs=[hbm] * 23,
        out_specs=(vmem, vmem, vmem),
        scratch_shapes=[
            pltpu.SMEM((HEADS, CACHE), F32), pltpu.VMEM((TOK, D), BF16), pltpu.VMEM((1, TOK), jnp.int32), pltpu.VMEM((1, TOK), jnp.int32),
            pltpu.VMEM((TOK, SRC), jnp.int32), pltpu.VMEM((3, 2, D), F32), pltpu.VMEM((EXP, D), F32),
            pltpu.VMEM((2, TOK, WID, SRC), BF16), pltpu.VMEM((2, TOK, WID, SRC), BF16),
            pltpu.VMEM((2, 3 * WID, D), BF16), pltpu.VMEM((2, WID, D), BF16),
            pltpu.VMEM((2, WID, D), BF16), pltpu.VMEM((2, WID, D), BF16),
            pltpu.VMEM((D, D), BF16), pltpu.VMEM((D, D), BF16), pltpu.VMEM((D, D), BF16),
            pltpu.VMEM((2, D, D), BF16), pltpu.VMEM((2, D, D), BF16), pltpu.VMEM((2, D, D), BF16),
            pltpu.VMEM((HEADS, CACHE, TOK), F32), pltpu.VMEM((HEADS, CACHE, TOK), F32),
            pltpu.VMEM((HALF * 8, SRC), F32), pltpu.VMEM((HALF * 8, SRC), BF16), pltpu.VMEM((HALF, WID), F32),
            pltpu.VMEM((6, TOK, D), BF16), pltpu.VMEM((6, 2, 3, ROWS, D), BF16), pltpu.VMEM((6, TOK, D), BF16),
            pltpu.VMEM((EXP * CAP, D), BF16), pltpu.VMEM((TOK, EXP * CAP), BF16),
            pltpu.VMEM((2, 4, CAP, D), BF16), pltpu.VMEM((2, 4, CAP, D), BF16), pltpu.VMEM((EXP * CAP, D), BF16),
            pltpu.VMEM((TOK, TOK), F32),
            dma((40,)), dma((6, 2, 3)), dma((6, 2, 3)), dma((6, 2, 3)), dma((6, 2, 3)),
            dma((2, 3)), dma((2, 3)), dma((2, 3)), dma((2, 3)),
        ],
        compiler_params=pltpu.CompilerParams(collective_id=0, has_side_effects=True, vmem_limit_bytes=VMEM_LIMIT),
        name="decode",
    )(rel_bias, hidden, write_pos.reshape(1, TOK), expert_idx.reshape(1, TOK), enc_mask, jnp.transpose(norm_scale, (1, 0, 2)), router.T,
      k_t, v_t, ck_t, cv_t, swap(w_query), swap(w_key), swap(w_value), w_out, swap(w_cross_query), w_cross_out,
      dense_gate, dense_up, dense_down, exp_gate, exp_up, exp_down)
    h_new, k_new, v_new = pl.pallas_call(
        store, out_shape=out_shape, in_specs=[vmem] * 3, out_specs=(hbm, hbm, hbm),
        scratch_shapes=[dma((3,))], compiler_params=pltpu.CompilerParams(vmem_limit_bytes=1 << 20), name="store")(*outs)
    back = lambda c: jnp.transpose(c, (0, 4, 1, 2, 3))
    return h_new, back(k_new), back(v_new)


def solution(mesh):
    batch = ('dp', 'ep')
    row_spec = P(batch, None)
    vec_spec = P(batch)
    cache_spec = P(None, batch, 'tp', None, None)
    col_spec = P(None, None, 'tp')
    out_rows = P(None, 'tp', None)
    in_specs = (row_spec, vec_spec, row_spec, vec_spec, cache_spec, cache_spec, cache_spec, cache_spec, P('tp', None), P(), col_spec, col_spec, col_spec, out_rows, col_spec, out_rows, P(None, 'tp'), P(None, 'tp'), P('tp', None), P(), P('ep', None, 'tp'), P('ep', None, 'tp'), P('ep', 'tp', None))
    out_specs = (row_spec, cache_spec, cache_spec)
    return jax.shard_map(decode_body, mesh=mesh, in_specs=in_specs, out_specs=out_specs, check_vma=False)
```

time: 113 us -> 89.7 us (0.79)
  Pallas kernels: 104 us -> 88.7 us
  local copies, waits for them, and re-layouts: 8.14 us -> 0 us
    pallas_call x1 -> x2, Pallas kernels: 104 us -> 88.7 us  [the longest x1 86 us: decode_body(): pl.pallas_call(kernel, out_shape=tuple((pltpu.VMEM(o.shape, o.dtype) for...]
    unnamed x5 -> x0, local copies, waits for them, and re-layouts: 8.14 us -> none
where the time goes in v2:
time: 89.7 us; the launch traced here: 89.6 us
  Pallas kernels  88.7 us (99%)
    pallas_call x1, Pallas kernels, decode_body(): pl.pallas_call(kernel, out_shape=tuple((pltpu.VMEM(o.shape, o.dtype) for...  86 us
    pallas_call x1, Pallas kernels, decode_body(): pl.pallas_call(store, out_shape=out_shape, in_specs=[vmem] * 3, out_specs...  2.78 us

profile of v2, /device:TPU:0, one launch (start us, length us, event | category | flops | bytes accessed | tf_op | source)
XLA Modules:
  0.0 89.6 jit_solution(17033378978660909375)
XLA Ops:
  0.6 86.0 %decode.1 = (bf16[128,768]{1,0:T(8,128)(2,1)S(1)}, bf16[2,3,32,64,128]{4,3,2,1,0:T(8,128)(2,1)S(1)}, bf16[2,3,32,64,128]{4,3,2,1,0:T(8,128)(2,1)S(1)}) custom-call(f32[3,32]{1,0:T(4,128)} %bias_h.1, bf16[128,768]{1,0:T(8,128)(2,1)} %hid_h.1, s32[1,128]{1,0:T(1,128)} %bitcast.28, s32[1,128]{1,0:T(1,128)} %bitcast.29, s32[128,128]{1,0:T(8,128)} %mask_h.1, ...), custom_call_target="tpu_custom_call" | custom-call | tf_op jit(solution)/shard_map/decode/pallas_call | solution.py:353
  86.6 2.8 %store.1 = (bf16[128,768]{1,0:T(8,128)(2,1)}, bf16[2,3,32,64,128]{4,3,2,1,0:T(8,128)(2,1)}, bf16[2,3,32,64,128]{4,3,2,1,0:T(8,128)(2,1)}) custom-call(bf16[128,768]{1,0:T(8,128)(2,1)S(1)} %get-tuple-element.9.h_v, bf16[2,3,32,64,128]{4,3,2,1,0:T(8,128)(2,1)S(1)} %get-tuple-element.10.k_v, bf16[2,3,32,64,128]{4,3,2,1,0:T(8,128)(2,1)S(1)} %get-tuple-element.11.v_v), custom_call_target="tpu_custom_call" | custom-call | tf_op jit(solution)/shard_map/store/pallas_call | solution.py:380
